TPU v7x, 512 devices: a whole 4x8x8 slice. The times are simulated.
512 devices in a mesh: row: 16 (over x_hi, z), col: 32 (over y, x_lo, core).
Axes of the slice: x: 4 (x_hi: 2, x_lo: 2; x = x_hi * 2 + x_lo), y: 8, z: 8, core: 2. Of those that a mesh axis runs over, the one named last changes fastest.
Arguments:
- raw_records: bfloat16 [2048, 768], P(('row', 'col')), may hold values from -6 to 6
- filter_taps: float32 [129], replicated, may hold values from -0.5 to 0.5
- lag_picks: int32 [2048, 2048], P('row', 'col'), may hold values from -2 to 2
- pair_valid: int32 [2048, 2048], P('row', 'col'), may hold values 0 or 1
- clock_offset: float32 [2048], P(('row', 'col')), may hold values from -12 to 12
- clock_drift: float32 [2048], P(('row', 'col')), may hold values from -3 to 3
- var_offset: float32 [2048], P(('row', 'col')), may hold values from 0.5 to 2
- cov_cross: float32 [2048], P(('row', 'col')), may hold values from -0.4 to 0.4
- var_drift: float32 [2048], P(('row', 'col')), may hold values from 0.5 to 2
Outputs:
- pair_misfit: float32 [2048, 2048], P('row', 'col')
- new_offset: float32 [2048], P(('row', 'col'))
- new_drift: float32 [2048], P(('row', 'col'))
- new_var_offset: float32 [2048], P(('row', 'col'))
- new_cov_cross: float32 [2048], P(('row', 'col'))
- new_var_drift: float32 [2048], P(('row', 'col'))
All inputs are finite; a program needn't handle non-finite values. No bound on the sum of `pair_valid` on one device may be relied on, other than what follows from the above.
Results may differ from a plain program's by a relative error of at most 0.0008.
Values may be sent and summed in bfloat16 or wider, within the bound.
No kernel may reach another device: no remote copies, remote signals or barrier semaphores. Data moves between devices by JAX's collectives and lax.ppermute only.
A program may use at most 64 MiB of HBM per device.

v0:
```python
import math
import jax
import jax.numpy as jnp
from jax import lax
from jax.sharding import PartitionSpec as P

LAG = 2
EPS = 1e-06
RHO = 0.5
Q_OFFSET = 0.05
Q_DRIFT = 0.01


def whiten(raw_rows, filter_taps):
    signal = raw_rows.astype(jnp.float32)[:, None, :]
    kernel = filter_taps[None, None, :]
    filtered = lax.conv_general_dilated(
        signal,
        kernel,
        (1,),
        "VALID",
        dimension_numbers=("NCH", "OIH", "NCH"),
        precision=lax.Precision.HIGHEST,
    )[:, 0, :]
    scaling = jnp.sqrt(jnp.mean(filtered * filtered, axis=1, keepdims=True) + EPS)
    return (filtered / scaling).astype(jnp.bfloat16)


def fitted_lag(white_rows, column_white, pick_rows):
    window = white_rows.shape[1] - 128
    centre_rows = white_rows[:, 64 : 64 + window]
    before_lag = jnp.zeros(pick_rows.shape, jnp.float32)
    at_lag = jnp.zeros(pick_rows.shape, jnp.float32)
    after_lag = jnp.zeros(pick_rows.shape, jnp.float32)
    for shift in range(-LAG - 1, LAG + 2):
        shifted = column_white[:, 64 + shift : 64 + shift + window]
        correl = lax.dot_general(
            centre_rows, shifted, (((1,), (1,)), ((), ())), preferred_element_type=jnp.float32
        ) / math.sqrt(window)
        before_lag = before_lag + jnp.where(pick_rows - 1 == shift, correl, 0.0)
        at_lag = at_lag + jnp.where(pick_rows == shift, correl, 0.0)
        after_lag = after_lag + jnp.where(pick_rows + 1 == shift, correl, 0.0)
    spread = jnp.maximum(
        jnp.sqrt(before_lag * before_lag + at_lag * at_lag + after_lag * after_lag), 1.0
    )
    return pick_rows.astype(jnp.float32) + (after_lag - before_lag) / spread


def local(
    raw_records,
    filter_taps,
    lag_picks,
    pair_valid,
    clock_offset,
    clock_drift,
    var_offset,
    cov_cross,
    var_drift,
):
    per_device = raw_records.shape[0]
    rows_count = lax.axis_size("row")
    cols_count = lax.axis_size("col")
    stations = per_device * rows_count * cols_count
    offset_pred = clock_offset + clock_drift
    voff = var_offset + 2.0 * cov_cross + var_drift + Q_OFFSET
    vcross = cov_cross + var_drift
    vdrift = var_drift + Q_DRIFT
    everyone = lax.all_gather(offset_pred, ("row", "col"), axis=0, tiled=True)
    offset_grid = everyone.reshape(rows_count, cols_count, per_device)
    row_index = lax.axis_index("row")
    col_index = lax.axis_index("col")
    row_offsets = lax.dynamic_index_in_dim(offset_grid, row_index, 0, keepdims=False).reshape(-1)
    column_offsets = lax.dynamic_index_in_dim(offset_grid, col_index, 1, keepdims=False).reshape(-1)
    valid_float = pair_valid.astype(jnp.float32)
    own_white = whiten(raw_records, filter_taps)
    column_white = lax.all_gather(own_white, "row", axis=0, tiled=True)
    white_rows = lax.all_gather(own_white, "col", axis=0, tiled=True)
    count = white_rows.shape[0]
    pick_rows = lax.slice_in_dim(lag_picks, 0, count, axis=0)
    valid_rows = lax.slice_in_dim(valid_float, 0, count, axis=0)
    offset_rows = lax.slice_in_dim(row_offsets, 0, count, axis=0)
    lagged = fitted_lag(white_rows, column_white, pick_rows)
    pair_misfit = valid_rows * (lagged - offset_rows[:, None] + column_offsets[None, :])
    row_terms = (jnp.sum(pair_misfit, axis=1), jnp.sum(valid_float, axis=1))
    column_terms = (-jnp.sum(pair_misfit, axis=0), jnp.sum(valid_float, axis=0))
    row_whole = lax.psum((row_terms[0], row_terms[1]), "col")
    column_whole = lax.psum((column_terms[0], column_terms[1]), "row")
    row_misfit = lax.dynamic_slice_in_dim(row_whole[0], col_index * per_device, per_device, 0)
    row_pairs = lax.dynamic_slice_in_dim(row_whole[1], col_index * per_device, per_device, 0)
    column_misfit = lax.dynamic_slice_in_dim(column_whole[0], row_index * per_device, per_device, 0)
    column_pairs = lax.dynamic_slice_in_dim(column_whole[1], row_index * per_device, per_device, 0)
    innovation = row_misfit + column_misfit
    pairs = row_pairs + column_pairs
    denom = pairs * voff + RHO * stations
    share = innovation / denom
    new_offset = offset_pred + voff * share
    new_drift = clock_drift + vcross * share
    new_var_offset = voff - voff * voff * pairs / denom
    new_cov_cross = vcross - voff * vcross * pairs / denom
    new_var_drift = vdrift - vcross * vcross * pairs / denom
    return (pair_misfit, new_offset, new_drift, new_var_offset, new_cov_cross, new_var_drift)


def solution(mesh):
    in_specs = (
        P(("row", "col"), None),
        P(),
        P("row", "col"),
        P("row", "col"),
        P(("row", "col")),
        P(("row", "col")),
        P(("row", "col")),
        P(("row", "col")),
        P(("row", "col")),
    )
    out_specs = (
        P("row", "col"),
        P(("row", "col")),
        P(("row", "col")),
        P(("row", "col")),
        P(("row", "col")),
        P(("row", "col")),
    )
    return jax.shard_map(local, mesh=mesh, in_specs=in_specs, out_specs=out_specs, check_vma=False)
```

profile of v0, /device:TPU:1, one launch (start us, length us, event | category | flops | bytes accessed | tf_op | source)
XLA Modules:
  0.0 324.8 jit_solution(12213304597258253916)
XLA Ops:
  0.6 0.0 copy-start.2
  0.7 0.0 copy-start.6
  0.7 0.6 copy-done.2
  1.3 0.0 copy-done.6
  1.3 0.1 fusion.20
  1.4 106.1 %all-reduce = f32[2048]{0:T(1024)S(1)} all-reduce(f32[2048]{0:T(1024)S(1)} %get-tuple-element.19), channel_id=1, replica_groups=mesh['row'=16,'col'=32] {'row','col'}, use_global_device_ids=true, to_apply=%add | all-reduce | flops 2048 | bytes 16384
  107.5 0.3 reshape.27
  107.8 0.1 sub.33
  107.9 0.0 copy-start.1
  107.9 0.1 add.174
  108.0 0.6 copy-done.1
  108.6 0.4 copy.20
  109.0 0.0 copy-start.5
  109.0 0.7 copy-done.5
  109.7 0.1 copy.21
  109.8 49.0 %fusion.21 = f32[4,1,640]{0,1,2:T(1,128)S(1)} fusion(bf16[4,1,768]{0,1,2:T(2,128)(2,1)S(1)} %copy.20, f32[1,1,129]{1,0,2:T(1,128)S(1)} %copy.21), kind=kOutput, calls=%fused_computation.51 | convolution fusion | flops 3962880 | bytes 16900 | tf_op jit(solution)/shard_map/conv_general_dilated | solution.py:17
  158.8 0.1 multiply_reduce_fusion
  159.0 0.1 copy.22
  159.1 33.0 %all-gather = bf16[32,4,640]{2,1,0:T(4,128)(2,1)S(1)} all-gather(bf16[1,4,640]{2,1,0:T(4,128)(2,1)S(1)} %copy.22), channel_id=1, replica_groups=mesh['row'=16,'col'=32] {'col'}, dimensions={0}, use_global_device_ids=true | all-gather | bytes 168960 | tf_op jit(solution)/shard_map/all_gather | solution.py:77
  192.1 30.2 %all-gather.1 = bf16[16,4,640]{2,1,0:T(4,128)(2,1)S(1)} all-gather(bf16[1,4,640]{2,1,0:T(4,128)(2,1)S(1)} %copy.22), channel_id=1, replica_groups=mesh['row'=16,'col'=32] {'row'}, dimensions={0}, use_global_device_ids=true | all-gather | bytes 87040 | tf_op jit(solution)/shard_map/all_gather | solution.py:76
  222.3 0.2 convolution_multiply_fusion.6
  222.6 0.3 convolution_multiply_fusion.5
  222.8 0.3 convolution_multiply_fusion.4
  223.1 0.3 convolution_multiply_fusion.3
  223.3 0.3 convolution_multiply_fusion.2
  223.6 0.0 copy-start
  223.6 0.0 copy-start.8
  223.6 0.2 convolution_multiply_fusion.1
  223.8 0.5 copy-done
  224.3 0.0 copy-done.8
  224.4 1.0 fusion.19
  225.4 0.1 convert_reduce_fusion.1
  225.5 30.2 %all-reduce.2 = (f32[64]{0:T(128)S(1)}, f32[64]{0:T(128)S(1)}) all-reduce(f32[64]{0:T(128)S(1)} %neg.3, f32[64]{0:T(128)S(1)} %get-tuple-element.7), channel_id=1, replica_groups=mesh['row'=16,'col'=32] {'row'}, use_global_device_ids=true, to_apply=%region_4.5 | all-reduce | flops 128 | bytes 1024 | tf_op jit(solution)/shard_map/psum | solution.py:87
  255.7 66.7 %all-reduce.1 = (f32[128]{0:T(128)S(1)}, f32[128]{0:T(128)S(1)}) all-reduce(f32[128]{0:T(128)S(1)} %get-tuple-element.8, f32[128]{0:T(128)S(1)} %get-tuple-element.6), channel_id=1, replica_groups=mesh['row'=16,'col'=32] {'col'}, use_global_device_ids=true, to_apply=%region_2.3 | all-reduce | flops 256 | bytes 2048 | tf_op jit(solution)/shard_map/psum | solution.py:86
  322.4 0.0 copy-start.3
  322.4 0.0 copy-start.4
  322.4 0.0 copy-start.7
  322.4 0.6 copy-done.3
  323.0 0.0 copy-done.4
  323.1 0.0 copy-done.7
  323.1 0.6 divide_subtract_fusion
  323.7 0.6 multiply_add_fusion
  324.3 0.5 multiply_add_fusion.1
  (8 shorter events, 0.2 us)
Async XLA Ops:
  0.6 0.7 copy-start.2
  0.7 0.7 copy-start.6
  107.9 0.7 copy-start.1
  109.0 0.7 copy-start.5
  223.6 0.8 copy-start
  223.6 0.8 copy-start.8
  322.4 0.7 copy-start.3
  322.4 0.7 copy-start.4
  322.4 0.7 copy-start.7
where the time goes:
time: 325 us
  blocking collectives  266 us (82%)
  matrix products  51.5 us (16%)
  local copies, waits for them, and re-layouts  4.3 us (1%)
    unnamed x1, blocking collectives  106 us
    psum x1, blocking collectives, local(): row_whole = lax.psum((row_terms[0], row_terms[1]), 'col')  66.7 us
    conv_general_dilated x1, matrix products, whiten(): lax.conv_general_dilated(signal, kernel, (1,), 'VALID', dimension_numbers...  49 us
    all_gather x1, blocking collectives, local(): white_rows = lax.all_gather(own_white, 'col', axis=0, tiled=True)  33 us
    all_gather x1, blocking collectives, local(): column_white = lax.all_gather(own_white, 'row', axis=0, tiled=True)  30.2 us
    psum x1, blocking collectives, local(): column_whole = lax.psum((column_terms[0], column_terms[1]), 'row')  30.2 us

commit v1 on v0

--- a/solution.py
+++ b/solution.py
@@ -73,7 +73,10 @@
     column_offsets = lax.dynamic_index_in_dim(offset_grid, col_index, 1, keepdims=False).reshape(-1)
     valid_float = pair_valid.astype(jnp.float32)
     own_white = whiten(raw_records, filter_taps)
-    column_white = lax.all_gather(own_white, "row", axis=0, tiled=True)
+    count_2 = lax.axis_size("row")
+    tiles = jnp.stack([own_white for _ in range(count_2)])
+    tiles = lax.all_to_all(tiles, "row", split_axis=0, concat_axis=0)
+    column_white = jnp.concatenate(tiles, axis=0)
     white_rows = lax.all_gather(own_white, "col", axis=0, tiled=True)
     count = white_rows.shape[0]
     pick_rows = lax.slice_in_dim(lag_picks, 0, count, axis=0)

time: 325 us -> 298 us (0.917)
  blocking collectives: 266 us -> 224 us
  starting transfers between devices: 0 us -> 13.4 us
    all_gather x1 -> x0, blocking collectives: 30.2 us -> none  [local(): column_white = lax.all_gather(own_white, 'row', axis=0, tiled=True)]
    all_to_all x0 -> x1, starting transfers between devices: none -> 13.4 us  [local(): tiles = lax.all_to_all(tiles, 'row', split_axis=0, concat_axis=0)]
    unnamed x1, blocking collectives: 106 us -> 99 us
    psum x1, blocking collectives: 66.7 us -> 59.7 us  [local(): row_whole = lax.psum((row_terms[0], row_terms[1]), 'col')]
  transfers between devices with their start and end apart: 0 -> 1, of which waited for: 0 -> 0; matrix products, arithmetic and copies ran while one was open for 0% -> 0% of each run, Pallas kernels for 0% -> 0%
where the time goes in v1:
time: 298 us; the launch traced here: 297 us
  blocking collectives  224 us (75%)
  matrix products  51.5 us (17%)
  starting transfers between devices  13.4 us (4%)
  local copies, waits for them, and re-layouts  5.69 us (2%)
    unnamed x1, blocking collectives  99 us
    psum x1, blocking collectives, local(): row_whole = lax.psum((row_terms[0], row_terms[1]), 'col')  59.7 us
    conv_general_dilated x1, matrix products, whiten(): lax.conv_general_dilated(signal, kernel, (1,), 'VALID', dimension_numbers...  49 us
    all_gather x1, blocking collectives, local(): white_rows = lax.all_gather(own_white, 'col', axis=0, tiled=True)  33.1 us
    psum x1, blocking collectives, local(): column_whole = lax.psum((column_terms[0], column_terms[1]), 'row')  31.8 us
    all_to_all x1, starting transfers between devices, local(): tiles = lax.all_to_all(tiles, 'row', split_axis=0, concat_axis=0)  13.4 us
  transfers between devices with their start and end apart: 1, of which 0 were waited for; matrix products, arithmetic and copies ran while one was open for 0% of the time, Pallas kernels for 0%

profile of v1, /device:TPU:1, one launch (start us, length us, event | category | flops | bytes accessed | tf_op | source)
XLA Modules:
  0.0 297.1 jit_solution(11659150843311396388)
XLA Ops:
  0.6 1.1 copy.21
  1.7 0.0 copy-start.4
  1.7 0.7 copy-done.4
  2.4 0.1 copy.22
  2.5 49.0 %fusion.20 = f32[4,1,640]{0,1,2:T(1,128)S(1)} fusion(bf16[4,1,768]{0,1,2:T(2,128)(2,1)S(1)} %copy.21, f32[1,1,129]{1,0,2:T(1,128)S(1)} %copy.22), kind=kOutput, calls=%fused_computation.50 | convolution fusion | flops 3962880 | bytes 16900 | tf_op jit(solution)/shard_map/conv_general_dilated | solution.py:17
  51.5 0.1 multiply_reduce_fusion
  51.7 0.1 copy.24
  51.8 0.7 stack.2
  52.4 13.4 %all-to-all-start = ((bf16[16,4,640]{2,1,0:T(4,128)(2,1)}), bf16[16,4,640]{2,1,0:T(4,128)(2,1)S(1)}, u32[]{:S(2)}, u32[]{:S(2)}) async-start(bf16[16,4,640]{2,1,0:T(4,128)(2,1)} %stack.2), calls=%async_computation | async-start | bytes 163840 | tf_op jit(solution)/shard_map/all_to_all | solution.py:78
  65.9 0.1 copy.23
  66.0 0.0 copy-start.1
  66.1 0.0 copy-start.5
  66.1 0.6 copy-done.1
  66.7 0.0 copy-done.5
  66.7 0.1 fusion.19
  66.8 99.0 %all-reduce = f32[2048]{0:T(1024)S(1)} all-reduce(f32[2048]{0:T(1024)S(1)} %get-tuple-element.19), channel_id=1, replica_groups=mesh['row'=16,'col'=32] {'row','col'}, use_global_device_ids=true, to_apply=%add | all-reduce | flops 2048 | bytes 16384
  165.9 0.3 reshape.40
  166.1 33.1 %all-gather = bf16[32,4,640]{2,1,0:T(4,128)(2,1)S(1)} all-gather(bf16[1,4,640]{2,1,0:T(4,128)(2,1)S(1)} %copy.23), channel_id=1, replica_groups=mesh['row'=16,'col'=32] {'col'}, dimensions={0}, use_global_device_ids=true | all-gather | bytes 168960 | tf_op jit(solution)/shard_map/all_gather | solution.py:80
  199.2 0.0 copy-start
  199.2 0.1 sub.33
  199.4 0.1 add.174
  199.5 0.5 copy-done
  200.0 0.1 convert_reduce_fusion.1
  200.1 0.0 all-to-all-done
  200.1 0.2 convolution_multiply_fusion.6
  200.4 0.3 convolution_multiply_fusion.5
  200.6 0.3 convolution_multiply_fusion.4
  200.9 0.3 convolution_multiply_fusion.3
  201.1 0.3 convolution_multiply_fusion.2
  201.4 0.0 copy-start.7
  201.4 0.2 convolution_multiply_fusion.1
  201.7 0.5 copy-done.7
  202.2 1.0 fusion.18
  203.2 31.8 %all-reduce.2 = (f32[64]{0:T(128)S(1)}, f32[64]{0:T(128)S(1)}) all-reduce(f32[64]{0:T(128)S(1)} %neg.3, f32[64]{0:T(128)S(1)} %get-tuple-element.7), channel_id=1, replica_groups=mesh['row'=16,'col'=32] {'row'}, use_global_device_ids=true, to_apply=%region_4.5 | all-reduce | flops 128 | bytes 1024 | tf_op jit(solution)/shard_map/psum | solution.py:90
  235.0 59.7 %all-reduce.1 = (f32[128]{0:T(128)S(1)}, f32[128]{0:T(128)S(1)}) all-reduce(f32[128]{0:T(128)S(1)} %get-tuple-element.8, f32[128]{0:T(128)S(1)} %get-tuple-element.6), channel_id=1, replica_groups=mesh['row'=16,'col'=32] {'col'}, use_global_device_ids=true, to_apply=%region_2.3 | all-reduce | flops 256 | bytes 2048 | tf_op jit(solution)/shard_map/psum | solution.py:89
  294.8 0.0 copy-start.2
  294.8 0.0 copy-start.3
  294.8 0.0 copy-start.6
  294.8 0.6 copy-done.2
  295.4 0.0 copy-done.3
  295.4 0.0 copy-done.6
  295.4 0.6 divide_subtract_fusion
  296.0 0.6 multiply_add_fusion
  296.6 0.5 multiply_add_fusion.1
  (9 shorter events, 0.2 us)
Async XLA Ops:
  1.7 0.7 copy-start.4
  52.4 147.7 %all-to-all-start = ((bf16[16,4,640]{2,1,0:T(4,128)(2,1)}), bf16[16,4,640]{2,1,0:T(4,128)(2,1)S(1)}, u32[]{:S(2)}, u32[]{:S(2)}) async-start(bf16[16,4,640]{2,1,0:T(4,128)(2,1)} %stack.2), calls=%async_computation | async-start | bytes 163840 | tf_op jit(solution)/shard_map/all_to_all | solution.py:78
  66.0 0.7 copy-start.1
  66.1 0.7 copy-start.5
  199.2 0.8 copy-start
  201.4 0.8 copy-start.7
  294.8 0.7 copy-start.2
  294.8 0.7 copy-start.3
  294.8 0.7 copy-start.6
